TPU v7x, 128 devices: a whole 4x4x4 slice. The times are simulated.
128 devices in a mesh: nodes: 128 (over z, y, x, core).
Axes of the slice: x: 4, y: 4, z: 4, core: 2. Of those that a mesh axis runs over, the one named last changes fastest.
Arguments:
- adjacency: bfloat16 [16384, 16384], P('nodes')
- features: bfloat16 [16384, 1433], P('nodes')
- w_hidden: float32 [1433, 16], replicated
- w_output: float32 [16, 7], replicated
- labels: int32 [16384], P('nodes')
- train_mask: int32 [16384], P('nodes')
- block_mask: int32 [128, 128], replicated
Outputs:
- output 1: float32 [], replicated
- output 2: float32 [1433, 16], replicated
- output 3: float32 [16, 7], replicated
All inputs are finite; a program needn't handle non-finite values.
Results may differ from a plain program's by a relative error of at most 0.001.
Values are sent between devices in bfloat16 or wider.
A program may use at most 1 GiB of HBM per device.

v0:
```python
import jax
import jax.numpy as jnp
from jax import lax
from jax.sharding import PartitionSpec as P

AXIS_NAME = 'nodes'
ROW_CONTRACT = (((0,), (0,)), ((), ()))
LAST_CONTRACT = (((1,), (1,)), ((), ()))


def gather_masked(local_vals, mask_row):
    gathered = lax.all_gather(local_vals, AXIS_NAME, axis=0, tiled=False)
    gathered = gathered * mask_row.astype(local_vals.dtype)[:, None, None]
    return gathered.reshape(-1, local_vals.shape[-1])


def transpose_product_scatter(adj_rows, local_grad, mask_row):
    width = local_grad.shape[-1]
    contrib = lax.dot_general(adj_rows, local_grad, ROW_CONTRACT, preferred_element_type=jnp.float32)
    contrib = contrib.reshape(mask_row.shape[0], -1, width) * mask_row.astype(jnp.float32)[:, None, None]
    return lax.psum_scatter(contrib.reshape(-1, width), AXIS_NAME, scatter_dimension=0, tiled=True)


def device_step(adj_rows, feat_rows, w_hidden, w_output, labels, train_mask, block_mask):
    dev_index = lax.axis_index(AXIS_NAME)
    mask_row = lax.dynamic_index_in_dim(block_mask, dev_index, axis=0, keepdims=False)
    w_hidden_bf = w_hidden.astype(jnp.bfloat16)
    w_output_bf = w_output.astype(jnp.bfloat16)
    proj_one = jnp.dot(feat_rows, w_hidden_bf, preferred_element_type=jnp.float32).astype(jnp.bfloat16)
    agg_one = jnp.dot(adj_rows, gather_masked(proj_one, mask_row), preferred_element_type=jnp.float32)
    hidden = jnp.maximum(agg_one, 0.0).astype(jnp.bfloat16)
    proj_two = jnp.dot(hidden, w_output_bf, preferred_element_type=jnp.float32).astype(jnp.bfloat16)
    logits = jnp.dot(adj_rows, gather_masked(proj_two, mask_row), preferred_element_type=jnp.float32)
    label_weight = train_mask.astype(jnp.float32)
    log_norm = jax.nn.logsumexp(logits, axis=-1)
    one_hot = (labels[:, None] == jnp.arange(logits.shape[-1])[None, :]).astype(jnp.float32)
    picked = jnp.sum(logits * one_hot, axis=-1)
    totals = lax.psum(jnp.stack([jnp.sum(label_weight), jnp.sum(label_weight * (log_norm - picked))]), AXIS_NAME)
    label_count = totals[0]
    mean_loss = totals[1] / label_count
    probabilities = jnp.exp(logits - log_norm[:, None])
    grad_logits = ((probabilities - one_hot) * (label_weight / label_count)[:, None]).astype(jnp.bfloat16)
    grad_proj_two = transpose_product_scatter(adj_rows, grad_logits, mask_row).astype(jnp.bfloat16)
    grad_w_output = lax.psum(lax.dot_general(hidden, grad_proj_two, ROW_CONTRACT, preferred_element_type=jnp.float32), AXIS_NAME)
    grad_hidden = lax.dot_general(grad_proj_two, w_output_bf, LAST_CONTRACT, preferred_element_type=jnp.float32)
    grad_agg = jnp.where(agg_one > 0, grad_hidden, 0.0).astype(jnp.bfloat16)
    grad_proj_one = transpose_product_scatter(adj_rows, grad_agg, mask_row).astype(jnp.bfloat16)
    grad_w_hidden = lax.psum(lax.dot_general(feat_rows, grad_proj_one, ROW_CONTRACT, preferred_element_type=jnp.float32), AXIS_NAME)
    return mean_loss, grad_w_hidden, grad_w_output


def solution(mesh):
    row_spec = P(AXIS_NAME, None)
    vec_spec = P(AXIS_NAME)
    return jax.shard_map(device_step, mesh=mesh, in_specs=(row_spec, row_spec, P(), P(), vec_spec, vec_spec, P()), out_specs=(P(), P(), P()), check_vma=False)
```

profile of v0, /device:TPU:1, one launch (start us, length us, event | category | flops | bytes accessed | tf_op | source)
XLA Modules:
  0.0 1599.7 jit_solution(995651929995067692)
XLA Ops:
  7.2 0.0 copy-start
  7.2 0.0 copy-start.2
  7.2 0.0 reduce-scatter.3.cloned.1.call-start
  7.2 0.9 copy-done
  8.2 1.1 convolution_convert_fusion
  9.2 39.3 %all-gather = bf16[16384,16]{0,1:T(8,128)(2,1)S(1)} all-gather(bf16[128,16]{0,1:T(8,128)(2,1)S(1)} %convolution_convert_fusion), channel_id=2, replica_groups=mesh['nodes'=128] {'nodes'}, dimensions={0}, use_global_device_ids=true | all-gather | bytes 528384 | tf_op jit(solution)/shard_map/all_gather | solution.py:12
  48.5 0.1 copy.10
  48.6 0.0 copy-start.1
  48.6 0.8 convert_bitcast_fusion
  49.4 0.1 bitcast_multiply_fusion
  49.6 0.0 copy-start.4
  49.6 0.0 copy-start.5
  49.6 3.7 fusion.3
  53.3 0.0 copy-done.2
  53.3 0.1 convolution_convert_fusion.1
  53.4 33.3 %all-gather.1 = bf16[16384,7]{0,1:T(8,128)(2,1)S(1)} all-gather(bf16[128,7]{0,1:T(8,128)(2,1)S(1)} %convolution_convert_fusion.1), channel_id=3, replica_groups=mesh['nodes'=128] {'nodes'}, dimensions={0}, use_global_device_ids=true | all-gather | bytes 231168 | tf_op jit(solution)/shard_map/all_gather | solution.py:12
  86.8 0.1 fusion.9
  86.8 0.0 copy-done.1
  86.9 1.2 fusion.38
  88.1 0.0 copy-done.4
  88.1 0.0 copy-done.5
  88.1 0.6 convert_reduce_fusion
  88.7 1.4 pad_maximum_fusion
  90.1 63.8 %psum.21 = f32[2]{0:T(128)S(1)} all-reduce(f32[2]{0:T(128)S(1)} %pad_maximum_fusion), channel_id=1, replica_groups=mesh['nodes'=128] {'nodes'}, use_global_device_ids=true, to_apply=%region_5.6 | all-reduce | flops 2 | bytes 16 | tf_op jit(solution)/shard_map/psum | solution.py:38
  153.9 0.6 fusion.37
  154.5 0.1 broadcast_bitcast_fusion
  154.5 0.7 convert_divide_fusion
  155.2 3.6 fusion.1
  158.8 0.0 reduce-scatter.3.cloned.1.call-update
  158.9 0.0 reduce-scatter.5.cloned.1.call-start
  158.9 635.8 %reduce-scatter.3.cloned.1.call-done = f32[128,7]{0,1:T(8,128)} async-done(((f32[16384,7]{0,1:T(8,128)}), f32[128,7]{0,1:T(8,128)}) %reduce-scatter.3.cloned.1.call-update) | async-done | bytes 3600 | tf_op jit(solution)/shard_map/reduce_scatter | solution.py:21
  794.7 0.0 copy-start.3
  794.7 4.0 fusion
  798.7 0.0 reduce-scatter.5.cloned.1.call-update
  798.8 0.0 all-reduce.2.cloned.1.call-start
  800.1 638.5 %reduce-scatter.5.cloned.1.call-done = f32[128,16]{0,1:T(8,128)} async-done(((f32[16384,16]{0,1:T(8,128)}), f32[128,16]{0,1:T(8,128)}) %reduce-scatter.5.cloned.1.call-update) | async-done | bytes 8208 | tf_op jit(solution)/shard_map/reduce_scatter | solution.py:21
  1438.7 1.6 convolution_bitcast_fusion
  1440.2 0.0 all-reduce.2.cloned.1.call-update
  1440.3 0.0 copy-done.3
  1440.3 0.1 fusion.27
  1440.4 69.1 %psum.23 = f32[16,7]{0,1:T(8,128)} all-reduce(f32[16,7]{0,1:T(8,128)S(1)} %fusion.27), channel_id=1, replica_groups=mesh['nodes'=128] {'nodes'}, use_global_device_ids=true, to_apply=%region_9.10 | all-reduce | flops 112 | bytes 896 | tf_op jit(solution)/shard_map/psum | solution.py:44
  1509.5 81.0 %all-reduce.2.cloned.1.call-done = f32[1433,16]{0,1:T(8,128)} async-done(((f32[1433,16]{0,1:T(8,128)}), f32[1433,16]{0,1:T(8,128)}) %all-reduce.2.cloned.1.call-update) | async-done | bytes 91728 | tf_op jit(solution)/shard_map/psum | solution.py:48
  1590.5 1.5 copy.26
  (2 shorter events, 0.0 us)
Async XLA Ops:
  7.2 1.0 copy-start
  7.2 46.1 %copy-start.2 = (f32[16,7]{0,1:T(8,128)S(1)}, f32[16,7]{0,1:T(8,128)}, u32[]{:S(2)}) copy-start(f32[16,7]{0,1:T(8,128)} %param.10) | copy-start | bytes 1348
  7.2 787.5 %reduce-scatter.3.cloned.1.call-start = ((), (), s32[]{:S(2)}) async-start(), calls=%async_computation.2 | async-start | bytes 528384 | tf_op jit(solution)/shard_map/reduce_scatter | solution.py:21
  48.6 38.3 %copy-start.1 = (bf16[128,16384]{1,0:T(8,128)(2,1)S(1)}, bf16[128,16384]{1,0:T(8,128)(2,1)}, u32[]{:S(2)}) copy-start(bf16[128,16384]{1,0:T(8,128)(2,1)} %param.7) | copy-start | bytes 12582916
  49.6 38.5 %copy-start.4 = (s32[128]{0:T(128)S(1)}, s32[128]{0:T(128)}, u32[]{:S(2)}) copy-start(s32[128]{0:T(128)} %param.11) | copy-start | bytes 1540
  49.6 38.5 %copy-start.5 = (s32[128]{0:T(128)S(1)}, s32[128]{0:T(128)}, u32[]{:S(2)}) copy-start(s32[128]{0:T(128)} %param.12) | copy-start | bytes 1540
  158.9 1279.8 %reduce-scatter.5.cloned.1.call-start = ((), (), s32[]{:S(2)}) async-start(), calls=%async_computation.3 | async-start | bytes 1056768 | tf_op jit(solution)/shard_map/reduce_scatter | solution.py:21
  794.7 645.6 %copy-start.3 = (f32[128,7]{0,1:T(8,128)S(1)}, f32[128,7]{0,1:T(8,128)}, u32[]{:S(2)}) copy-start(f32[128,7]{0,1:T(8,128)} %reduce-scatter.3.cloned.1.call-done) | copy-start | bytes 10756
  798.8 791.7 %all-reduce.2.cloned.1.call-start = ((), (), s32[]{:S(2)}) async-start(), calls=%async_computation.4 | async-start | bytes 196608 | tf_op jit(solution)/shard_map/psum | solution.py:48
Sparse Core Ops, SparseCore 0:
  159.0 635.6 reduce-scatter.2
  798.9 639.7 reduce-scatter.4
  1444.0 146.4 all-reduce.1
where the time goes:
time: 1600 us
  waiting for transfers between devices  1360 us (85%)
  blocking collectives  205 us (13%)
  between operations  16.3 us (1%)
    reduce_scatter x2, waiting for transfers between devices, transpose_product_scatter(): lax.psum_scatter(contrib.reshape(-1, width), AXIS_NAME, scatter_dimension...  1270 us
    psum x1, waiting for transfers between devices, device_step(): lax.psum(lax.dot_general(feat_rows, grad_proj_one, ROW_CONTRACT, preferre...  81 us
    all_gather x2, blocking collectives, gather_masked(): gathered = lax.all_gather(local_vals, AXIS_NAME, axis=0, tiled=False)  72.6 us
    psum x1, blocking collectives, device_step(): lax.psum(lax.dot_general(hidden, grad_proj_two, ROW_CONTRACT, preferred_e...  69.1 us
    psum x1, blocking collectives, device_step(): lax.psum(jnp.stack([jnp.sum(label_weight), jnp.sum(label_weight * (log_no...  63.8 us
  transfers between devices with their start and end apart: 3, of which 3 were waited for; matrix products, arithmetic and copies ran while one was open for 0% of the time, Pallas kernels for 0%

commit v1 on v0

v1 whole, which is shorter than its diff:
```python
import functools

import jax
import jax.numpy as jnp
from jax import lax
from jax.experimental import pallas as pl
from jax.experimental.pallas import tpu as pltpu
from jax.sharding import PartitionSpec as P

AXIS = 'nodes'
MESH = pl.DeviceIdType.MESH
BF = jnp.bfloat16
F32 = jnp.float32
NT = (((1,), (1,)), ((), ()))
TN = (((0,), (0,)), ((), ()))
B = 128
CLS = 7


def kernel(R, adj, x_t, wh_t, wo_t, labels, tmask, bmask, gwh_out, gwo_out, loss_out,
           a_v, x_v, wh_v, wo_v, wo_pad, lab_v, tm_v, bm_s, y1_v, y2_v, z_v, z_rx,
           g_v, e_v, p_v, p_rx, q_v, q_rx, part, part_rx, acc, acc_rx, fin_rx,
           load_sem, a_sem, a_send, d_send, d_recv, send_sem, recv_sem, ar_send, ar_recv):
    NC = R * R * R
    f_in = x_v.shape[0]
    fpad = part.shape[2] - B
    me = lax.axis_index(AXIS)
    core = lax.rem(me, 2)
    chip = lax.div(me, 2)
    cx = lax.rem(chip, R)
    cy = lax.rem(lax.div(chip, R), R)
    cz = lax.div(chip, R * R)
    partner = chip * 2 + (1 - core)

    def peer(dz, dy, dx):
        tz = lax.rem(cz + dz, R)
        ty = lax.rem(cy + dy, R)
        tx = lax.rem(cx + dx, R)
        return (tz * R + ty) * R + tx

    def peer_k(k):
        return peer(lax.div(k, R * R), lax.rem(lax.div(k, R), R), lax.rem(k, R))

    def blk(t):
        return pl.ds(pl.multiple_of(t * B, B), B)

    small = [
        pltpu.make_async_copy(x_t, x_v, load_sem.at[0]),
        pltpu.make_async_copy(wh_t, wh_v, load_sem.at[1]),
        pltpu.make_async_copy(wo_t, wo_v, load_sem.at[2]),
        pltpu.make_async_copy(labels, lab_v, load_sem.at[3]),
        pltpu.make_async_copy(tmask, tm_v, load_sem.at[4]),
        pltpu.make_async_copy(bmask.at[pl.ds(pl.multiple_of(lax.div(2 * chip, 8) * 8, 8), 8), :], bm_s, load_sem.at[5]),
    ]
    for c in small:
        c.start()

    barrier = pltpu.get_barrier_semaphore()

    def greet(k, _):
        pl.semaphore_signal(barrier, inc=1, device_id=(peer_k(k) * 2 + core,), device_id_type=MESH)
        return 0

    lax.fori_loop(1, NC, greet, 0)
    pl.semaphore_signal(barrier, inc=1, device_id=(partner,), device_id_type=MESH)

    my_rows = pl.ds(pl.multiple_of(core * B, B), B)

    def load_a(t, _):
        pltpu.make_async_copy(adj.at[:, blk(2 * t + core)], a_v.at[my_rows, blk(t)], a_sem.at[0]).start()
        return 0

    lax.fori_loop(0, NC, load_a, 0)

    wo_pad[...] = jnp.zeros_like(wo_pad)
    g_v[...] = jnp.zeros_like(g_v)
    part[...] = jnp.zeros_like(part)
    small[0].wait()
    small[1].wait()
    y1 = jnp.dot(wh_v[...].astype(BF), x_v[...], preferred_element_type=F32).astype(BF)
    y1_v[:, blk(chip)] = y1

    pl.semaphore_wait(barrier, NC)

    def gather_start(buf, i):
        def send(k, _):
            pltpu.make_async_remote_copy(
                src_ref=buf.at[:, blk(chip)], dst_ref=buf.at[:, blk(chip)], send_sem=send_sem.at[i], recv_sem=recv_sem.at[i],
                device_id=(peer_k(k) * 2 + core,), device_id_type=MESH).start()
            return 0

        lax.fori_loop(1, NC, send, 0)

    def wait_all(ref, sem):
        pltpu.make_async_copy(ref, ref, sem).wait()

    gather_start(y1_v, 0)

    def swap_a(t, _):
        pltpu.make_async_remote_copy(
            src_ref=adj.at[:, blk(2 * t + 1 - core)], dst_ref=a_v.at[my_rows, blk(t)], send_sem=a_send, recv_sem=a_sem.at[1],
            device_id=(partner,), device_id_type=MESH).start()
        return 0

    lax.fori_loop(0, NC, swap_a, 0)
    for c in small[2:]:
        c.wait()
    wo_pad[0:CLS, :] = wo_v[...]
    wo_bf = wo_pad[...].astype(BF)
    wait_all(a_v.at[0:B, :], a_sem.at[0])
    wait_all(a_v.at[0:B, :], a_sem.at[1])

    row0 = lax.rem(2 * chip, 8)

    def mask_block(t, _):
        for h in range(2):
            m = bm_s[row0 + h, 2 * t + core].astype(F32)
            m_vec = jnp.full((B, B), m, F32).astype(BF)
            a_v[h * B:(h + 1) * B, blk(t)] = a_v[h * B:(h + 1) * B, blk(t)] * m_vec
        return 0

    lax.fori_loop(0, NC, mask_block, 0)

    def to_partner(src, dst, i):
        return pltpu.make_async_remote_copy(src_ref=src, dst_ref=dst, send_sem=d_send.at[i], recv_sem=d_recv.at[i],
                                            device_id=(partner,), device_id_type=MESH)

    def others(buf):
        return buf.at[:, 0:(NC - 1) * B]

    wait_all(others(y1_v), recv_sem.at[0])
    zp = lax.dot_general(y1_v[...], a_v[...], NT, preferred_element_type=F32)
    z_v[0, 0] = zp[:, 0:B]
    z_v[0, 1] = zp[:, B:2 * B]
    zc = to_partner(z_v.at[0, 1 - core], z_rx.at[0], 0)
    zc.start()
    zc.wait()
    z1 = z_v[0, core] + z_rx[0]
    h_bf = jnp.maximum(z1, 0.0).astype(BF)
    rows16 = lax.broadcasted_iota(jnp.int32, (16, B), 0)
    m_row = tm_v[...].astype(F32)
    y2 = jnp.dot(wo_bf, h_bf, preferred_element_type=F32)
    y2 = jnp.where(rows16 == CLS, m_row, y2)
    y2_v[:, blk(chip)] = y2.astype(BF)
    gather_start(y2_v, 1)

    wait_all(others(y2_v), recv_sem.at[1])
    zp = lax.dot_general(y2_v[...], a_v[...], NT, preferred_element_type=F32)
    cnt = jnp.zeros((16, B), F32)
    for t in range(NC):
        cnt = cnt + y2_v[:, t * B:(t + 1) * B].astype(F32)
    z_v[1, 0] = jnp.where(rows16 == CLS, cnt, zp[:, 0:B])
    z_v[1, 1] = jnp.where(rows16 == CLS, cnt, zp[:, B:2 * B])
    zc2 = to_partner(z_v.at[1, 1 - core], z_rx.at[1], 1)
    zc2.start()
    zc2.wait()
    z2 = (z_v[1, core] + z_rx[1])[0:8, :]
    rows8 = lax.broadcasted_iota(jnp.int32, (8, B), 0)
    count = jnp.sum(z2[CLS:CLS + 1, :], axis=1, keepdims=True)
    valid = rows8 < CLS
    zmax = jnp.max(jnp.where(valid, z2, -jnp.inf), axis=0, keepdims=True)
    esum = jnp.sum(jnp.where(valid, jnp.exp(z2 - zmax), 0.0), axis=0, keepdims=True)
    log_norm = jnp.log(esum) + zmax
    hot = rows8 == lab_v[...]
    picked = jnp.sum(jnp.where(hot, z2, 0.0), axis=0, keepdims=True)
    loss_part = jnp.sum(m_row * (log_norm - picked), axis=1, keepdims=True)
    prob = jnp.exp(jnp.where(valid, z2 - log_norm, 0.0))
    g = (prob - hot.astype(F32)) * (m_row / count)
    g = jnp.where(valid, g, 0.0)
    g_v[:, blk(core)] = jnp.concatenate([g, jnp.zeros_like(g)], axis=0).astype(BF)
    gc = to_partner(g_v.at[:, blk(core)], g_v.at[:, blk(core)], 2)
    gc.start()
    gc.wait()

    def scatter_product(lhs_v, rows, out_v, rx, i):
        lhs = lhs_v[...]
        W = R * B

        def one_group(dz, dy, first_x):
            base = (lax.rem(cz + dz, R) * R + lax.rem(cy + dy, R)) * R
            res = jnp.dot(lhs, a_v[:, pl.ds(pl.multiple_of(base * B, W), W)], preferred_element_type=F32)
            for j in range(R):
                out_v[base + j] = res[0:rows, j * B:(j + 1) * B]
            for dx in range(first_x, R):
                t = base + lax.rem(cx + dx, R)
                pltpu.make_async_remote_copy(
                    src_ref=out_v.at[t], dst_ref=rx.at[chip], send_sem=send_sem.at[i], recv_sem=recv_sem.at[i],
                    device_id=(t * 2 + core,), device_id_type=MESH).start()

        def step(k, _):
            one_group(lax.div(k, R), lax.rem(k, R), 0)
            return 0

        lax.fori_loop(1, R * R, step, 0)
        one_group(0, 0, 1)
        rx[chip] = out_v[chip]
        wait_all(rx.at[0:NC - 1], recv_sem.at[i])
        return jnp.sum(rx[...], axis=0)

    d2 = scatter_product(g_v, 8, p_v, p_rx, 2).astype(BF)
    d2_16 = jnp.concatenate([d2.astype(F32), jnp.zeros((8, B), F32)], axis=0).astype(BF)
    gh = lax.dot_general(wo_bf, d2_16, TN, preferred_element_type=F32)
    e_v[:, blk(core)] = jnp.where(z1 > 0, gh, 0.0).astype(BF)
    ec = to_partner(e_v.at[:, blk(core)], e_v.at[:, blk(core)], 3)
    ec.start()
    gwo = lax.dot_general(d2_16, h_bf, NT, preferred_element_type=F32)
    tail = jnp.where(rows8 == CLS, loss_part, 0.0)
    for h in range(2):
        part[h, :, fpad:] = tail
        part[h, :, fpad:fpad + 16] = jnp.where(rows8[:, 0:16] == CLS, loss_part, gwo[0:8, :])
    ec.wait()
    d1 = scatter_product(e_v, 16, q_v, q_rx, 3).astype(BF)
    gwh = lax.dot_general(d1, x_v[...], NT, preferred_element_type=F32)
    part[0, :, 0:f_in] = gwh[0:8]
    part[1, :, 0:f_in] = gwh[8:16]
    pc = to_partner(part.at[1 - core], part_rx, 4)
    pc.start()
    pc.wait()
    acc[0] = part[core] + part_rx[...]

    tiles = acc.shape[2] // B
    cuts = [0, tiles // 3 * B, 2 * (tiles // 3) * B, tiles * B]
    coords = (cz, cy, cx)

    def axis_peer(ax, d):
        off = [0, 0, 0]
        off[ax] = d
        return peer(*off) * 2 + core

    def cols(s):
        return slice(cuts[s], cuts[s + 1])

    def launch(p, s):
        ax = (p + s) % 3
        for d in range(1, R):
            pltpu.make_async_remote_copy(
                src_ref=acc.at[p, :, cols(s)], dst_ref=acc_rx.at[p, coords[ax], :, cols(s)],
                send_sem=ar_send.at[p, s], recv_sem=ar_recv.at[p, s],
                device_id=(axis_peer(ax, d),), device_id_type=MESH).start()
        acc_rx[p, coords[ax], :, cols(s)] = acc[p, :, cols(s)]

    for s in range(3):
        launch(0, s)
    for p in range(3):
        for s in range(3):
            wait_all(acc_rx.at[p, 0:R - 1, :, cols(s)], ar_recv.at[p, s])
            tot = acc_rx[p, 0, :, cols(s)]
            for r in range(1, R):
                tot = tot + acc_rx[p, r, :, cols(s)]
            acc[p + 1, :, cols(s)] = tot
            if p < 2:
                launch(p + 1, s)
    fc = to_partner(acc.at[3], fin_rx, 5)
    fc.start()
    gwo_out[...] = acc[3, 0:CLS, fpad:fpad + 16]
    loss_out[...] = acc[3, CLS:CLS + 1, fpad:fpad + 1] / count
    gwh_out[pl.ds(pl.multiple_of(core * 8, 8), 8), :] = acc[3, :, 0:f_in]
    fc.wait()
    gwh_out[pl.ds(pl.multiple_of((1 - core) * 8, 8), 8), :] = fin_rx[:, 0:f_in]

    wait_all(a_v.at[0:B, :], a_send)
    wait_all(others(y1_v), send_sem.at[0])
    wait_all(others(y2_v), send_sem.at[1])
    wait_all(p_rx.at[0:NC - 1], send_sem.at[2])
    wait_all(q_rx.at[0:NC - 1], send_sem.at[3])
    for p in range(3):
        for s in range(3):
            wait_all(acc_rx.at[p, 0:R - 1, :, cols(s)], ar_send.at[p, s])


def device_step(R, adj, feat, w_hidden, w_output, labels, train_mask, block_mask):
    NC = R * R * R
    f_in, hid = w_hidden.shape
    fpad = -(-f_in // B) * B
    any_spec = pl.BlockSpec(memory_space=pl.ANY)
    vmem_spec = pl.BlockSpec(memory_space=pltpu.VMEM)
    gwh, gwo, loss = pl.pallas_call(
        functools.partial(kernel, R),
        out_shape=(jax.ShapeDtypeStruct((hid, f_in), F32), jax.ShapeDtypeStruct((CLS, hid), F32), jax.ShapeDtypeStruct((1, 1), F32)),
        in_specs=[any_spec] * 7,
        out_specs=(vmem_spec, vmem_spec, vmem_spec),
        scratch_shapes=[
            pltpu.VMEM((2 * B, NC * B), BF),
            pltpu.VMEM((f_in, B), BF),
            pltpu.VMEM((hid, f_in), F32),
            pltpu.VMEM((CLS, hid), F32),
            pltpu.VMEM((16, hid), F32),
            pltpu.VMEM((1, B), jnp.int32),
            pltpu.VMEM((1, B), jnp.int32),
            pltpu.SMEM((8, block_mask.shape[1]), jnp.int32),
            pltpu.VMEM((hid, NC * B), BF),
            pltpu.VMEM((16, NC * B), BF),
            pltpu.VMEM((2, 2, 16, B), F32),
            pltpu.VMEM((2, 16, B), F32),
            pltpu.VMEM((16, 2 * B), BF),
            pltpu.VMEM((16, 2 * B), BF),
            pltpu.VMEM((NC, 8, B), F32),
            pltpu.VMEM((NC, 8, B), F32),
            pltpu.VMEM((NC, 16, B), F32),
            pltpu.VMEM((NC, 16, B), F32),
            pltpu.VMEM((2, 8, fpad + B), F32),
            pltpu.VMEM((8, fpad + B), F32),
            pltpu.VMEM((4, 8, fpad + B), F32),
            pltpu.VMEM((3, R, 8, fpad + B), F32),
            pltpu.VMEM((8, fpad + B), F32),
            pltpu.SemaphoreType.DMA((6,)),
            pltpu.SemaphoreType.DMA((2,)),
            pltpu.SemaphoreType.DMA,
            pltpu.SemaphoreType.DMA((6,)),
            pltpu.SemaphoreType.DMA((6,)),
            pltpu.SemaphoreType.DMA((4,)),
            pltpu.SemaphoreType.DMA((4,)),
            pltpu.SemaphoreType.DMA((3, 3)),
            pltpu.SemaphoreType.DMA((3, 3)),
        ],
        compiler_params=pltpu.CompilerParams(collective_id=0, has_side_effects=True, vmem_limit_bytes=60 * 1024 * 1024),
        name='gcn_step',
    )(adj, feat.T, w_hidden.T, w_output.T, labels.reshape(1, -1), train_mask.reshape(1, -1), block_mask)
    return loss[0, 0], gwh.T, gwo.T


def solution(mesh):
    row_spec = P(AXIS, None)
    vec_spec = P(AXIS)
    R = 4 if mesh.shape[AXIS] == 128 else 2
    return jax.shard_map(functools.partial(device_step, R), mesh=mesh,
                         in_specs=(row_spec, row_spec, P(), P(), vec_spec, vec_spec, P()), out_specs=(P(), P(), P()), check_vma=False)
```

time: 1600 us -> 72.5 us (0.05)
  waiting for transfers between devices: 1360 us -> 0 us
  blocking collectives: 205 us -> 0 us
  Pallas kernels: 0 us -> 67.2 us
    reduce_scatter x2 -> x0, waiting for transfers between devices: 1270 us -> none  [transpose_product_scatter(): lax.psum_scatter(contrib.reshape(-1, width), AXIS_NAME, scatter_dimension...]
    psum x2 -> x0, blocking collectives: 133 us -> none  [the longest x1 69.1 us: device_step(): lax.psum(lax.dot_general(hidden, grad_proj_two, ROW_CONTRACT, preferred_e...]
    psum x1 -> x0, waiting for transfers between devices: 81 us -> none  [device_step(): lax.psum(lax.dot_general(feat_rows, grad_proj_one, ROW_CONTRACT, preferre...]
    all_gather x2 -> x0, blocking collectives: 72.6 us -> none  [gather_masked(): gathered = lax.all_gather(local_vals, AXIS_NAME, axis=0, tiled=False)]
    pallas_call x0 -> x1, Pallas kernels: none -> 67.2 us  [device_step(): pl.pallas_call(functools.partial(kernel, R), out_shape=(jax.ShapeDtypeStr...]
  transfers between devices with their start and end apart: 3 -> 0, of which waited for: 3 -> 0; matrix products, arithmetic and copies ran while one was open for 0% -> 0% of each run, Pallas kernels for 0% -> 0%
where the time goes in v1:
time: 72.5 us; the launch traced here: 72.4 us
  Pallas kernels  67.2 us (93%)
  local copies, waits for them, and re-layouts  2.81 us (4%)
  between operations  2.33 us (3%)
    pallas_call x1, Pallas kernels, device_step(): pl.pallas_call(functools.partial(kernel, R), out_shape=(jax.ShapeDtypeStr...  67.2 us
    unnamed x2, local copies, waits for them, and re-layouts  2.81 us

profile of v1, /device:TPU:1, one launch (start us, length us, event | category | flops | bytes accessed | tf_op | source)
XLA Modules:
  0.0 72.4 jit_solution(7505071897764767879)
XLA Ops:
  0.6 67.2 %gcn_step.1 = (f32[16,1433]{1,0:T(8,128)}, f32[7,16]{1,0:T(8,128)}, f32[1,1]{1,0:T(1,128)}) custom-call(bf16[128,16384]{1,0:T(8,128)(2,1)} %adj.1, bf16[1433,128]{1,0:T(8,128)(2,1)} %bitcast.8, f32[16,1433]{1,0:T(8,128)} %bitcast.10, f32[7,16]{1,0:T(8,128)} %bitcast.11, s32[1,128]{1,0:T(1,128)} %bitcast.13, s32[1,128]{1,0:T(1,128)} %bitcast.14, s32[128,128]{1,0:T(8,128)} %bmask.1), custom_call_target="tpu_custom_call" | custom-call | tf_op jit(solution)/shard_map/gcn_step/pallas_call | solution.py:277
  68.4 1.5 %copy.14 = f32[1433,16]{0,1:T(8,128)} copy(f32[1433,16]{0,1:T(8,128)} %bitcast.9) | data formatting | bytes 183424
  70.0 1.3 %copy.15 = f32[16,7]{0,1:T(8,128)} copy(f32[16,7]{0,1:T(8,128)} %bitcast.12) | data formatting | bytes 896

commit v2 on v1

v2 whole, which is shorter than its diff:
```python
import functools

import jax
import jax.numpy as jnp
from jax import lax
from jax.experimental import pallas as pl
from jax.experimental.pallas import tpu as pltpu
from jax.sharding import PartitionSpec as P

AXIS = 'nodes'
MESH = pl.DeviceIdType.MESH
BF = jnp.bfloat16
F32 = jnp.float32
NT = (((1,), (1,)), ((), ()))
TN = (((0,), (0,)), ((), ()))
B = 128
CLS = 7


def kernel(R, adj, x_t, wh_t, wo_t, labels, tmask, bmask, gwh_out, gwo_out, loss_out,
           a_v, x_v, wh_v, wo_v, wo_pad, lab_v, tm_v, bm_s, y1_v, y2_v, z1_v, z1_rx, z2_v, z2_rx,
           g_v, e_v, p_v, p_rx, q_v, q_rx, part, rx0, acc1, rx1, acc2, rx2,
           load_sem, a_sem, a_send, d_send, d_recv, send_sem, recv_sem, ar_send, ar_recv):
    NC = R * R * R
    SL = R * R
    FAR = (2, 3, 1, 0) if R == 4 else (1, 0)
    NEAR = FAR[::-1]
    f_in = x_v.shape[0]
    width = part.shape[2]
    fpad = width - B
    me = lax.axis_index(AXIS)
    core = lax.rem(me, 2)
    other = 1 - core
    chip = lax.div(me, 2)
    cx = lax.rem(chip, R)
    cy = lax.rem(lax.div(chip, R), R)
    cz = lax.div(chip, SL)
    coords = (cz, cy, cx)
    partner = chip * 2 + other
    tz = [lax.rem(cz + d, R) * SL for d in range(R)]
    ty = [lax.rem(cy + d, R) * R for d in range(R)]
    tx = [lax.rem(cx + d, R) for d in range(R)]
    offsets = [(dz, dy, dx) for dz in FAR for dy in FAR for dx in FAR if dz or dy or dx]
    dz2 = [t * 2 + core for t in tz]
    dy2 = [t * 2 for t in ty]
    dx2 = [t * 2 for t in tx]

    def dev(dz, dy, dx):
        return dz2[dz] + dy2[dy] + dx2[dx]

    def blk(t):
        return pl.ds(pl.multiple_of(t * B, B), B)

    def rcopy(src, dst, ss, rs, device):
        return pltpu.make_async_remote_copy(src_ref=src, dst_ref=dst, send_sem=ss, recv_sem=rs, device_id=(device,), device_id_type=MESH)

    def wait_all(ref, sem):
        pltpu.make_async_copy(ref, ref, sem).wait()

    def ring_dev(ax, d, h):
        off = [0, 0, 0]
        off[ax] = d
        return (tz[off[0]] + ty[off[1]] + tx[off[2]]) * 2 + h

    barrier = pltpu.get_barrier_semaphore()
    for o in offsets:
        pl.semaphore_signal(barrier, inc=1, device_id=(dev(*o),), device_id_type=MESH)
    pl.semaphore_signal(barrier, inc=1, device_id=(partner,), device_id_type=MESH)
    for ax in range(3):
        for d in range(1, R):
            pl.semaphore_signal(barrier, inc=1, device_id=(ring_dev(ax, d, other),), device_id_type=MESH)

    mine = blk(core)
    theirs = blk(other)
    small = [
        pltpu.make_async_copy(x_t, x_v, load_sem.at[0]),
        pltpu.make_async_copy(wh_t, wh_v, load_sem.at[1]),
        pltpu.make_async_copy(bmask.at[pl.ds(pl.multiple_of(lax.div(2 * chip, 8) * 8, 8), 8), :], bm_s, load_sem.at[2]),
        pltpu.make_async_copy(wo_t, wo_v, load_sem.at[3]),
        pltpu.make_async_copy(labels, lab_v.at[:, mine], load_sem.at[4]),
        pltpu.make_async_copy(tmask, tm_v.at[:, mine], load_sem.at[5]),
    ]
    for c in small:
        c.start()

    def load_a(t, _):
        pltpu.make_async_copy(adj.at[:, blk(2 * t + core)], a_v.at[mine, blk(t)], a_sem.at[0]).start()
        return 0

    lax.fori_loop(0, NC, load_a, 0, unroll=4)
    wo_pad[...] = jnp.zeros_like(wo_pad)
    part[...] = jnp.zeros_like(part)
    small[0].wait()
    small[1].wait()
    y1_v[:, blk(chip)] = jnp.dot(wh_v[...].astype(BF), x_v[...], preferred_element_type=F32).astype(BF)
    for c in small[2:]:
        c.wait()
    wo_pad[0:CLS, :] = wo_v[...]
    wo_bf = wo_pad[...].astype(BF)

    row0 = lax.rem(2 * chip, 8)

    def mask_rows(h):
        def step(t, _):
            m = jnp.full((B, B), bm_s[row0 + h, 2 * t + core].astype(F32), F32).astype(BF)
            a_v[blk(h), blk(t)] = a_v[blk(h), blk(t)] * m
            return 0

        lax.fori_loop(0, NC, step, 0, unroll=4)

    wait_all(a_v.at[0:B, :], a_sem.at[0])
    mask_rows(core)

    pl.semaphore_wait(barrier, NC + 3 * (R - 1))

    def gather_start(buf, i):
        src = buf.at[:, blk(chip)]
        for o in offsets:
            rcopy(src, src, send_sem.at[i], recv_sem.at[i, o[0]], dev(*o)).start()

    gather_start(y1_v, 0)

    def swap_a(t, _):
        rcopy(adj.at[:, blk(2 * t + other)], a_v.at[mine, blk(t)], a_send, a_sem.at[1], partner).start()
        return 0

    lax.fori_loop(0, NC, swap_a, 0, unroll=4)
    lc = rcopy(labels, lab_v.at[:, mine], d_send.at[3], d_recv.at[3], partner)
    mc = rcopy(tmask, tm_v.at[:, mine], d_send.at[4], d_recv.at[4], partner)
    lc.start()
    mc.start()
    wait_all(a_v.at[0:B, :], a_sem.at[1])
    mask_rows(other)

    def slab(dz):
        z = lax.rem(cz + R - dz, R)
        return pl.ds(pl.multiple_of(z * (SL * B), SL * B), SL * B)

    def wait_slab(buf, i, dz):
        n = SL if dz else SL - 1
        wait_all(buf.at[:, 0:n * B], recv_sem.at[i, dz])

    def prod(buf, rows, dz):
        return lax.dot_general(buf[:, slab(dz)], a_v[rows, slab(dz)], NT, preferred_element_type=F32)

    own = jnp.zeros((16, B), F32)
    far = jnp.zeros((16, B), F32)
    for dz in NEAR[:-1]:
        wait_slab(y1_v, 0, dz)
        far = far + prod(y1_v, theirs, dz)
        own = own + prod(y1_v, mine, dz)
    dz = NEAR[-1]
    wait_slab(y1_v, 0, dz)
    z1_v[...] = far + prod(y1_v, theirs, dz)
    zc = rcopy(z1_v, z1_rx, d_send.at[0], d_recv.at[0], partner)
    zc.start()
    own = own + prod(y1_v, mine, dz)
    zc.wait()
    z1 = own + z1_rx[...]
    h_bf = jnp.maximum(z1, 0.0).astype(BF)
    rows16 = lax.broadcasted_iota(jnp.int32, (16, B), 0)
    y2 = jnp.dot(wo_bf, h_bf, preferred_element_type=F32)
    y2 = jnp.where(rows16 == CLS, tm_v[:, mine].astype(F32), y2)
    y2_v[:, blk(chip)] = y2.astype(BF)
    gather_start(y2_v, 1)

    lc.wait()
    mc.wait()
    every = slice(0, 2 * B)
    both = jnp.zeros((16, 2 * B), F32)
    cnt = jnp.zeros((16, B), F32)

    def slab_count(dz, cnt):
        z = lax.rem(cz + R - dz, R)
        for t in range(SL):
            cnt = cnt + y2_v[:, blk(z * SL + t)].astype(F32)
        return cnt

    for dz in NEAR[:-1]:
        wait_slab(y2_v, 1, dz)
        both = both + prod(y2_v, every, dz)
        cnt = slab_count(dz, cnt)
    dz = NEAR[-1]
    wait_slab(y2_v, 1, dz)
    both = both + prod(y2_v, every, dz)
    cnt = slab_count(dz, cnt)
    for h in range(2):
        z2_v[:, h * B:(h + 1) * B] = jnp.where(rows16 == CLS, cnt, both[:, h * B:(h + 1) * B])
    zc2 = rcopy(z2_v, z2_rx, d_send.at[1], d_recv.at[1], partner)
    zc2.start()
    zc2.wait()
    z2 = (z2_v[...] + z2_rx[...])[0:8, :]
    rows8 = lax.broadcasted_iota(jnp.int32, (8, 2 * B), 0)
    lanes = lax.broadcasted_iota(jnp.int32, (1, 2 * B), 1)
    count = jnp.sum(z2[CLS:CLS + 1, 0:B], axis=1, keepdims=True)
    m_row = tm_v[...].astype(F32)
    valid = rows8 < CLS
    zmax = jnp.max(jnp.where(valid, z2, -jnp.inf), axis=0, keepdims=True)
    esum = jnp.sum(jnp.where(valid, jnp.exp(jnp.where(valid, z2 - zmax, 0.0)), 0.0), axis=0, keepdims=True)
    log_norm = jnp.log(esum) + zmax
    hot = rows8 == lab_v[...]
    picked = jnp.sum(jnp.where(hot, z2, 0.0), axis=0, keepdims=True)
    loss_row = jnp.where(lax.div(lanes, B) == core, m_row * (log_norm - picked), 0.0)
    loss_part = jnp.sum(loss_row, axis=1, keepdims=True)
    prob = jnp.exp(jnp.where(valid, z2 - log_norm, 0.0))
    g = (prob - hot.astype(F32)) * (m_row / count)
    g = jnp.where(valid, g, 0.0)
    g_v[...] = jnp.concatenate([g, jnp.zeros_like(g)], axis=0).astype(BF)

    def scatter_product(lhs_v, rows, out_v, rx, i):
        lhs = lhs_v[...]
        for dz in FAR:
            base = tz[dz]
            res = jnp.dot(lhs, a_v[:, pl.ds(pl.multiple_of(base * B, SL * B), SL * B)], preferred_element_type=F32)
            for j in range(SL):
                out_v[base + j] = res[0:rows, j * B:(j + 1) * B]
            for dy in FAR:
                for dx in FAR:
                    if dz or dy or dx:
                        rcopy(out_v.at[base + ty[dy] + tx[dx]], rx.at[chip], send_sem.at[i], recv_sem.at[i, 0], dev(dz, dy, dx)).start()
        rx[chip] = out_v[chip]

    def scatter_sum(rx, i):
        wait_all(rx.at[0:NC - 1], recv_sem.at[i, 0])
        return jnp.sum(rx[...], axis=0)

    scatter_product(g_v, 8, p_v, p_rx, 2)
    d2 = scatter_sum(p_rx, 2)
    d2_16 = jnp.concatenate([d2, jnp.zeros((8, B), F32)], axis=0).astype(BF)
    gh = lax.dot_general(wo_bf, d2_16, TN, preferred_element_type=F32)
    e_v[:, mine] = jnp.where(z1 > 0, gh, 0.0).astype(BF)
    ec = rcopy(e_v.at[:, mine], e_v.at[:, mine], d_send.at[2], d_recv.at[2], partner)
    ec.start()
    gwo = lax.dot_general(d2_16, h_bf, NT, preferred_element_type=F32)
    for h in range(2):
        part[h, :, fpad:fpad + 16] = jnp.where(rows8[:, 0:16] == CLS, loss_part, gwo[0:8, :])
    ec.wait()
    scatter_product(e_v, 16, q_v, q_rx, 3)
    d1 = scatter_sum(q_rx, 3).astype(BF)
    gwh = lax.dot_general(d1, x_v[...], NT, preferred_element_type=F32)
    part[0, :, 0:f_in] = gwh[0:8]
    part[1, :, 0:f_in] = gwh[8:16]

    third = width // B // 3 * B
    cuts = [slice(0, third), slice(third, 2 * third), slice(2 * third, width)]

    def launch(p, s):
        ax = (p + s) % 3
        c = cuts[s]
        me_ax = coords[ax]
        ss, rs = ar_send.at[p, s], ar_recv.at[p, s]
        for d in FAR:
            if p == 1:
                if d:
                    rcopy(acc1.at[:, c], rx1.at[me_ax, :, c], ss, rs, ring_dev(ax, d, core)).start()
                continue
            for h in (other, core):
                if d == 0 and h is core:
                    continue
                src = part.at[h, :, c] if p == 0 else acc2.at[:, c]
                slot = me_ax * 2 + core if p == 0 else core * R + me_ax
                rcopy(src, (rx0 if p == 0 else rx2).at[slot, :, c], ss, rs, ring_dev(ax, d, h)).start()
        if p == 0:
            rx0[me_ax * 2 + core, :, c] = part[core, :, c]
        elif p == 1:
            rx1[me_ax, :, c] = acc1[:, c]
        else:
            rx2[core * R + me_ax, :, c] = acc2[:, c]

    def total(rx, lo, n, c):
        tot = rx[lo, :, c]
        for r in range(1, n):
            tot = tot + rx[lo + r, :, c]
        return tot

    for s in range(3):
        launch(0, s)
    for s in range(3):
        c = cuts[s]
        wait_all(rx0.at[0:2 * R - 1, :, c], ar_recv.at[0, s])
        acc1[:, c] = total(rx0, 0, 2 * R, c)
        launch(1, s)
    for s in range(3):
        c = cuts[s]
        wait_all(rx1.at[0:R - 1, :, c], ar_recv.at[1, s])
        acc2[:, c] = total(rx1, 0, R, c)
        launch(2, s)
    for s in range(3):
        c = cuts[s]
        wait_all(rx2.at[0:2 * R - 1, :, c], ar_recv.at[2, s])
        end = min(c.stop, f_in)
        lo = total(rx2, 0, R, c)
        hi = total(rx2, R, R, c)
        gwh_out[0:8, c.start:end] = lo[:, 0:end - c.start]
        gwh_out[8:16, c.start:end] = hi[:, 0:end - c.start]
        if s == 2:
            tail = lo[:, fpad - c.start:]
            gwo_out[...] = tail[0:CLS, 0:16]
            loss_out[...] = tail[CLS:CLS + 1, 0:1] / count

    wait_all(a_v.at[0:B, :], a_send)
    wait_all(y1_v.at[:, 0:(NC - 1) * B], send_sem.at[0])
    wait_all(y2_v.at[:, 0:(NC - 1) * B], send_sem.at[1])
    wait_all(p_rx.at[0:NC - 1], send_sem.at[2])
    wait_all(q_rx.at[0:NC - 1], send_sem.at[3])
    for s in range(3):
        c = cuts[s]
        wait_all(rx0.at[0:2 * R - 1, :, c], ar_send.at[0, s])
        wait_all(rx1.at[0:R - 1, :, c], ar_send.at[1, s])
        wait_all(rx2.at[0:2 * R - 1, :, c], ar_send.at[2, s])


def device_step(R, adj, feat, w_hidden, w_output, labels, train_mask, block_mask):
    NC = R * R * R
    f_in, hid = w_hidden.shape
    fpad = -(-f_in // B) * B
    any_spec = pl.BlockSpec(memory_space=pl.ANY)
    vmem_spec = pl.BlockSpec(memory_space=pltpu.VMEM)
    gwh, gwo, loss = pl.pallas_call(
        functools.partial(kernel, R),
        out_shape=(pltpu.VMEM((hid, f_in), F32), pltpu.VMEM((CLS, hid), F32), pltpu.VMEM((1, 1), F32)),
        in_specs=[any_spec] * 7,
        out_specs=(vmem_spec, vmem_spec, vmem_spec),
        scratch_shapes=[
            pltpu.VMEM((2 * B, NC * B), BF),
            pltpu.VMEM((f_in, B), BF),
            pltpu.VMEM((hid, f_in), F32),
            pltpu.VMEM((CLS, hid), F32),
            pltpu.VMEM((16, hid), F32),
            pltpu.VMEM((1, 2 * B), jnp.int32),
            pltpu.VMEM((1, 2 * B), jnp.int32),
            pltpu.SMEM((8, block_mask.shape[1]), jnp.int32),
            pltpu.VMEM((hid, NC * B), BF),
            pltpu.VMEM((16, NC * B), BF),
            pltpu.VMEM((16, B), F32),
            pltpu.VMEM((16, B), F32),
            pltpu.VMEM((16, 2 * B), F32),
            pltpu.VMEM((16, 2 * B), F32),
            pltpu.VMEM((16, 2 * B), BF),
            pltpu.VMEM((16, 2 * B), BF),
            pltpu.VMEM((NC, 8, B), F32),
            pltpu.VMEM((NC, 8, B), F32),
            pltpu.VMEM((NC, 16, B), F32),
            pltpu.VMEM((NC, 16, B), F32),
            pltpu.VMEM((2, 8, fpad + B), F32),
            pltpu.VMEM((2 * R, 8, fpad + B), F32),
            pltpu.VMEM((8, fpad + B), F32),
            pltpu.VMEM((R, 8, fpad + B), F32),
            pltpu.VMEM((8, fpad + B), F32),
            pltpu.VMEM((2 * R, 8, fpad + B), F32),
            pltpu.SemaphoreType.DMA((6,)),
            pltpu.SemaphoreType.DMA((2,)),
            pltpu.SemaphoreType.DMA,
            pltpu.SemaphoreType.DMA((5,)),
            pltpu.SemaphoreType.DMA((5,)),
            pltpu.SemaphoreType.DMA((4,)),
            pltpu.SemaphoreType.DMA((4, R)),
            pltpu.SemaphoreType.DMA((3, 3)),
            pltpu.SemaphoreType.DMA((3, 3)),
        ],
        compiler_params=pltpu.CompilerParams(collective_id=0, has_side_effects=True, vmem_limit_bytes=60 * 1024 * 1024),
        name='gcn_step',
    )(adj, feat.T, w_hidden.T, w_output.T, labels.reshape(1, -1), train_mask.reshape(1, -1), block_mask)
    return loss[0, 0], gwh.T, gwo.T


def solution(mesh):
    row_spec = P(AXIS, None)
    vec_spec = P(AXIS)
    R = 4 if mesh.shape[AXIS] == 128 else 2
    return jax.shard_map(functools.partial(device_step, R), mesh=mesh,
                         in_specs=(row_spec, row_spec, P(), P(), vec_spec, vec_spec, P()), out_specs=(P(), P(), P()), check_vma=False)
```

time: 72.5 us -> 61.7 us (0.85)
  Pallas kernels: 67.2 us -> 58.4 us
  local copies, waits for them, and re-layouts: 2.81 us -> 1.24 us
    pallas_call x1, Pallas kernels: 67.2 us -> 58.4 us  [device_step(): pl.pallas_call(functools.partial(kernel, R), out_shape=(pltpu.VMEM((hid,...]
    unnamed x2, local copies, waits for them, and re-layouts: 2.81 us -> 1.24 us
where the time goes in v2:
time: 61.7 us; the launch traced here: 61.5 us
  Pallas kernels  58.4 us (95%)
  between operations  1.8 us (3%)
  local copies, waits for them, and re-layouts  1.24 us (2%)
    pallas_call x1, Pallas kernels, device_step(): pl.pallas_call(functools.partial(kernel, R), out_shape=(pltpu.VMEM((hid,...  58.4 us
    unnamed x2, local copies, waits for them, and re-layouts  1.24 us

profile of v2, /device:TPU:1, one launch (start us, length us, event | category | flops | bytes accessed | tf_op | source)
XLA Modules:
  0.0 61.5 jit_solution(13366971728400670157)
XLA Ops:
  0.6 58.4 %gcn_step.1 = (f32[16,1433]{1,0:T(8,128)S(1)}, f32[7,16]{1,0:T(8,128)S(1)}, f32[1,1]{1,0:T(1,128)S(1)}) custom-call(bf16[128,16384]{1,0:T(8,128)(2,1)} %adj.1, bf16[1433,128]{1,0:T(8,128)(2,1)} %bitcast.10, f32[16,1433]{1,0:T(8,128)} %bitcast.11, f32[7,16]{1,0:T(8,128)} %bitcast.12, s32[1,128]{1,0:T(1,128)} %bitcast.13, s32[1,128]{1,0:T(1,128)} %bitcast.14, ...), custom_call_target="tpu_custom_call" | custom-call | tf_op jit(solution)/shard_map/gcn_step/pallas_call | solution.py:319
  59.1 0.6 %copy.14 = f32[1433,16]{0,1:T(8,128)} copy(f32[1433,16]{0,1:T(8,128)S(1)} %bitcast.8) | data formatting | bytes 183424
  59.7 0.6 copy.15

commit v3 on v2

v3 whole, which is shorter than its diff:
```python
import functools

import jax
import jax.numpy as jnp
from jax import lax
from jax.experimental import pallas as pl
from jax.experimental.pallas import tpu as pltpu
from jax.sharding import PartitionSpec as P

AXIS = 'nodes'
MESH = pl.DeviceIdType.MESH
BF = jnp.bfloat16
F32 = jnp.float32
NT = (((1,), (1,)), ((), ()))
TN = (((0,), (0,)), ((), ()))
B = 128
CLS = 7


def tail_offset(f_in):
    return -(-f_in // 16) * 16


def kernel(R, adj, x_t, wh_t, wo_t, labels, tmask, bmask, out,
           a_v, x_v, wh_v, wo_v, wo_pad, lab_v, tm_v, bm_s, y1_v, y2_v, z1_v, z1_rx, z2_v, z2_rx,
           g_v, e_v, p_v, p_rx, q_v, q_rx, part, rx0, acc1, rx1, acc2, rx2,
           load_sem, a_sem, a_send, d_send, d_recv, send_sem, recv_sem, ar_send, ar_recv):
    NC = R * R * R
    SL = R * R
    FAR = (2, 3, 1, 0) if R == 4 else (1, 0)
    NEAR = FAR[::-1]
    f_in = x_v.shape[0]
    width = part.shape[2]
    toff = tail_offset(f_in)
    tail = slice(toff, toff + 16)
    me = lax.axis_index(AXIS)
    core = lax.rem(me, 2)
    other = 1 - core
    chip = lax.div(me, 2)
    cx = lax.rem(chip, R)
    cy = lax.rem(lax.div(chip, R), R)
    cz = lax.div(chip, SL)
    coords = (cz, cy, cx)
    partner = chip * 2 + other
    tz = [lax.rem(cz + d, R) * SL for d in range(R)]
    ty = [lax.rem(cy + d, R) * R for d in range(R)]
    tx = [lax.rem(cx + d, R) for d in range(R)]
    offsets = [(dz, dy, dx) for dz in FAR for dy in FAR for dx in FAR if dz or dy or dx]
    offsets.sort(key=lambda o: -sum(min(d, R - d) for d in o))
    tz_src = [lax.rem(cz + R - d, R) * SL for d in range(R)]
    ty_src = [lax.rem(cy + R - d, R) * R for d in range(R)]

    def rank_of(o):
        return max(sum(min(d, R - d) for d in o[:2]) - 1, 0)

    ranks = [[(dz, dy) for dz in range(R) for dy in range(R) if rank_of((dz, dy)) == r] for r in range(2 * (R // 2))]
    arrivals = [R * len(r) - (1 if (0, 0) in r else 0) for r in ranks]
    dz2 = [t * 2 + core for t in tz]
    dy2 = [t * 2 for t in ty]
    dx2 = [t * 2 for t in tx]

    def dev(dz, dy, dx):
        return dz2[dz] + dy2[dy] + dx2[dx]

    def blk(t):
        return pl.ds(pl.multiple_of(t * B, B), B)

    def rcopy(src, dst, ss, rs, device):
        return pltpu.make_async_remote_copy(src_ref=src, dst_ref=dst, send_sem=ss, recv_sem=rs, device_id=(device,), device_id_type=MESH)

    def wait_all(ref, sem):
        pltpu.make_async_copy(ref, ref, sem).wait()

    def ring_dev(ax, d, h):
        off = [0, 0, 0]
        off[ax] = d
        return (tz[off[0]] + ty[off[1]] + tx[off[2]]) * 2 + h

    barrier = pltpu.get_barrier_semaphore()
    for o in offsets:
        pl.semaphore_signal(barrier, inc=1, device_id=(dev(*o),), device_id_type=MESH)
    pl.semaphore_signal(barrier, inc=1, device_id=(partner,), device_id_type=MESH)
    for ax in range(3):
        for d in range(1, R):
            pl.semaphore_signal(barrier, inc=1, device_id=(ring_dev(ax, d, other),), device_id_type=MESH)

    mine = blk(core)
    theirs = blk(other)
    small = [
        pltpu.make_async_copy(x_t, x_v, load_sem.at[0]),
        pltpu.make_async_copy(wh_t, wh_v, load_sem.at[1]),
        pltpu.make_async_copy(bmask.at[pl.ds(pl.multiple_of(lax.div(2 * chip, 8) * 8, 8), 8), :], bm_s, load_sem.at[2]),
        pltpu.make_async_copy(wo_t, wo_v, load_sem.at[3]),
        pltpu.make_async_copy(labels, lab_v.at[:, mine], load_sem.at[4]),
        pltpu.make_async_copy(tmask, tm_v.at[:, mine], load_sem.at[5]),
    ]
    for c in small:
        c.start()

    def load_a(t, _):
        pltpu.make_async_copy(adj.at[:, blk(2 * t + core)], a_v.at[mine, blk(t)], a_sem.at[0]).start()
        return 0

    lax.fori_loop(0, NC, load_a, 0, unroll=4)
    wo_pad[...] = jnp.zeros_like(wo_pad)
    part[...] = jnp.zeros_like(part)
    small[0].wait()
    small[1].wait()
    y1_v[:, blk(chip)] = jnp.dot(wh_v[...].astype(BF), x_v[...], preferred_element_type=F32).astype(BF)
    for c in small[2:]:
        c.wait()
    wo_pad[0:CLS, :] = wo_v[...]
    wo_bf = wo_pad[...].astype(BF)

    row0 = lax.rem(2 * chip, 8)

    def mask_rows(h):
        def step(t, _):
            m = jnp.full((B, B), bm_s[row0 + h, 2 * t + core].astype(F32), F32).astype(BF)
            a_v[blk(h), blk(t)] = a_v[blk(h), blk(t)] * m
            return 0

        lax.fori_loop(0, NC, step, 0, unroll=4)

    wait_all(a_v.at[0:B, :], a_sem.at[0])
    mask_rows(core)

    pl.semaphore_wait(barrier, NC + 3 * (R - 1))

    def gather_start(buf, i):
        src = buf.at[:, blk(chip)]
        for o in offsets:
            rcopy(src, src, send_sem.at[i], recv_sem.at[i, rank_of(o)], dev(*o)).start()

    gather_start(y1_v, 0)

    def swap_a(t, _):
        rcopy(adj.at[:, blk(2 * t + other)], a_v.at[mine, blk(t)], a_send, a_sem.at[1], partner).start()
        return 0

    lax.fori_loop(0, NC, swap_a, 0, unroll=4)
    lc = rcopy(labels, lab_v.at[:, mine], d_send.at[3], d_recv.at[3], partner)
    mc = rcopy(tmask, tm_v.at[:, mine], d_send.at[4], d_recv.at[4], partner)
    lc.start()
    mc.start()
    wait_all(a_v.at[0:B, :], a_sem.at[1])
    mask_rows(other)

    def group(o):
        return pl.ds(pl.multiple_of((tz_src[o[0]] + ty_src[o[1]]) * B, R * B), R * B)

    def wait_rank(buf, i, rank):
        wait_all(buf.at[:, 0:arrivals[rank] * B], recv_sem.at[i, rank])

    def prod(buf, rank):
        left = jnp.concatenate([buf[:, group(o)] for o in rank], axis=1)
        halves = []
        for h in range(2):
            right = jnp.concatenate([a_v[h * B:(h + 1) * B, group(o)] for o in rank], axis=1)
            halves.append(lax.dot_general(left, right, NT, preferred_element_type=F32))
        return halves

    def gathered_product(buf, i, counted=False):
        cnt = jnp.zeros((buf.shape[0], B), F32)
        lo = jnp.zeros((buf.shape[0], B), F32)
        hi = jnp.zeros((buf.shape[0], B), F32)
        for rank in range(len(ranks)):
            wait_rank(buf, i, rank)
            p_lo, p_hi = prod(buf, ranks[rank])
            lo = lo + p_lo
            hi = hi + p_hi
            if counted:
                for o in ranks[rank]:
                    for x in range(R):
                        cnt = cnt + buf[:, blk(tz_src[o[0]] + ty_src[o[1]] + x)].astype(F32)
        return (lo, hi, cnt) if counted else (lo, hi)

    z1_v[0], z1_v[1] = gathered_product(y1_v, 0)
    zc = rcopy(z1_v.at[other], z1_rx, d_send.at[0], d_recv.at[0], partner)
    zc.start()
    zc.wait()
    z1 = z1_v[core] + z1_rx[...]
    h_bf = jnp.maximum(z1, 0.0).astype(BF)
    rows8 = lax.broadcasted_iota(jnp.int32, (8, 2 * B), 0)
    is_count = rows8[:, 0:B] == CLS
    y2 = jnp.dot(wo_bf, h_bf, preferred_element_type=F32)
    y2 = jnp.where(is_count, tm_v[:, mine].astype(F32), y2)
    y2_v[:, blk(chip)] = y2.astype(BF)
    gather_start(y2_v, 1)

    lc.wait()
    mc.wait()
    *both, cnt = gathered_product(y2_v, 1, counted=True)
    for h in range(2):
        z2_v[:, h * B:(h + 1) * B] = jnp.where(is_count, cnt, both[h])
    zc2 = rcopy(z2_v, z2_rx, d_send.at[1], d_recv.at[1], partner)
    zc2.start()
    zc2.wait()
    z2 = z2_v[...] + z2_rx[...]
    lanes = lax.broadcasted_iota(jnp.int32, (1, 2 * B), 1)
    count = jnp.sum(z2[CLS:CLS + 1, 0:B], axis=1, keepdims=True)
    m_row = tm_v[...].astype(F32)
    valid = rows8 < CLS
    zmax = jnp.max(jnp.where(valid, z2, -jnp.inf), axis=0, keepdims=True)
    esum = jnp.sum(jnp.where(valid, jnp.exp(jnp.where(valid, z2 - zmax, 0.0)), 0.0), axis=0, keepdims=True)
    log_norm = jnp.log(esum) + zmax
    hot = rows8 == lab_v[...]
    picked = jnp.sum(jnp.where(hot, z2, 0.0), axis=0, keepdims=True)
    loss_row = jnp.where(lax.div(lanes, B) == core, m_row * (log_norm - picked), 0.0)
    loss_part = jnp.sum(loss_row, axis=1, keepdims=True)
    prob = jnp.exp(jnp.where(valid, z2 - log_norm, 0.0))
    g = (prob - hot.astype(F32)) * (m_row / count)
    g_v[...] = jnp.where(valid, g, 0.0).astype(BF)

    def product(lhs, rings):
        cols = jnp.concatenate([a_v[:, pl.ds(pl.multiple_of((tz[o[0]] + ty[o[1]]) * B, R * B), R * B)] for o in rings], axis=1)
        return jnp.dot(lhs, cols, preferred_element_type=F32)

    def scatter_product(lhs_v, outs, chunks, send_block):
        lhs = lhs_v[...]
        for chunk in chunks:
            cut = (len(chunk) + 1) // 2
            for rings in (chunk[:cut], chunk[cut:]):
                if rings:
                    res = product(lhs, rings)
                    for n, o in enumerate(rings):
                        for j in range(R):
                            for h, out_v in enumerate(outs):
                                out_v[tz[o[0]] + ty[o[1]] + j] = res[h * 8:h * 8 + 8, (n * R + j) * B:(n * R + j + 1) * B]
            for o in offsets:
                if o[:2] in chunk:
                    send_block(0, o)

    def sender(outs, rxs, i):
        def send_block(h, o):
            t = tz[o[0]] + ty[o[1]] + tx[o[2]]
            rcopy(outs[h].at[t], rxs[h].at[chip], send_sem.at[i + h], recv_sem.at[i + h, 0], dev(*o)).start()

        return send_block

    def scatter_sum(rx, i):
        wait_all(rx.at[0:NC - 1], recv_sem.at[i, 0])
        return jnp.sum(rx[...], axis=0)

    by_rank = [list(r) for r in ranks[::-1]]
    if R == 4:
        by_rank = [by_rank[0] + by_rank[1], by_rank[2], by_rank[3]]
    by_z = [[(dz, dy) for dy in FAR] for dz in FAR]

    scatter_product(g_v, [p_v], by_rank, sender([p_v], [p_rx], 2))
    p_rx[chip] = p_v[chip]
    d2 = scatter_sum(p_rx, 2).astype(BF)
    gh = lax.dot_general(wo_bf, d2, TN, preferred_element_type=F32)
    e_v[:, mine] = jnp.where(z1 > 0, gh, 0.0).astype(BF)
    ec = rcopy(e_v.at[:, mine], e_v.at[:, mine], d_send.at[2], d_recv.at[2], partner)
    ec.start()
    gwo = lax.dot_general(d2, h_bf, NT, preferred_element_type=F32)
    ec.wait()
    q_vs = [q_v.at[h] for h in range(2)]
    q_rxs = [q_rx.at[h] for h in range(2)]
    send_q = sender(q_vs, q_rxs, 3)
    scatter_product(e_v, q_vs, by_z, send_q)
    for o in offsets:
        send_q(1, o)
    for h in range(2):
        q_rx[h, chip] = q_v[h, chip]

    tiles = width // B
    streams = 6 if tiles >= 6 else 3
    cuts = [slice(tiles * s // streams * B, tiles * (s + 1) // streams * B) for s in range(streams)]

    def launch_first(h, s):
        ax = s % 3
        c = cuts[s]
        slot = coords[ax] * 2 + core
        for d in FAR[:-1]:
            rcopy(part.at[h, :, c], rx0.at[slot, :, c], ar_send.at[0, s], ar_recv.at[0, s], ring_dev(ax, d, h)).start()

        @pl.when(core == h)
        def _():
            rx0[slot, :, c] = part[h, :, c]

        @pl.when(core != h)
        def _():
            rcopy(part.at[h, :, c], rx0.at[slot, :, c], ar_send.at[0, s], ar_recv.at[0, s], partner).start()

    def launch(p, s):
        ax = (p + s) % 3
        c = cuts[s]
        me_ax = coords[ax]
        ss, rs = ar_send.at[p, s], ar_recv.at[p, s]
        for d in FAR:
            if p == 1:
                if d:
                    rcopy(acc1.at[:, c], rx1.at[me_ax, :, c], ss, rs, ring_dev(ax, d, core)).start()
                continue
            for h in (other, core):
                if d or h is other:
                    rcopy(acc2.at[:, c], rx2.at[core * R + me_ax, :, c], ss, rs, ring_dev(ax, d, h)).start()
        if p == 1:
            rx1[me_ax, :, c] = acc1[:, c]
        else:
            rx2[core * R + me_ax, :, c] = acc2[:, c]

    def total(rx, lo, n, c):
        tot = rx[lo, :, c]
        for r in range(1, n):
            tot = tot + rx[lo + r, :, c]
        return tot

    for h in range(2):
        d1 = scatter_sum(q_rxs[h], 3 + h).astype(BF)
        part[h, :, 0:f_in] = lax.dot_general(d1, x_v[...], NT, preferred_element_type=F32)
        part[h, :, tail] = jnp.where(rows8[:, 0:16] == CLS, loss_part, gwo)
        for s in range(streams):
            launch_first(h, s)
    for s in range(streams):
        c = cuts[s]
        wait_all(rx0.at[0:2 * R - 1, :, c], ar_recv.at[0, s])
        acc1[:, c] = total(rx0, 0, 2 * R, c)
        launch(1, s)
    for s in range(streams):
        c = cuts[s]
        wait_all(rx1.at[0:R - 1, :, c], ar_recv.at[1, s])
        acc2[:, c] = total(rx1, 0, R, c)
        launch(2, s)
    for s in range(streams):
        c = cuts[s]
        wait_all(rx2.at[0:2 * R - 1, :, c], ar_recv.at[2, s])
        out[0:8, c] = total(rx2, 0, R, c)
        out[8:16, c] = total(rx2, R, R, c)
    out[15:16, tail] = jnp.broadcast_to(out[CLS:CLS + 1, toff:toff + 1] / count, (1, 16))

    wait_all(a_v.at[0:B, :], a_send)
    wait_all(y1_v.at[:, 0:(NC - 1) * B], send_sem.at[0])
    wait_all(y2_v.at[:, 0:(NC - 1) * B], send_sem.at[1])
    wait_all(p_rx.at[0:NC - 1], send_sem.at[2])
    for h in range(2):
        wait_all(q_rx.at[h, 0:NC - 1], send_sem.at[3 + h])
    for s in range(streams):
        c = cuts[s]
        wait_all(rx0.at[0:2 * R - 1, :, c], ar_send.at[0, s])
        wait_all(rx1.at[0:R - 1, :, c], ar_send.at[1, s])
        wait_all(rx2.at[0:2 * R - 1, :, c], ar_send.at[2, s])


def unpack(packed, gwh_out, gwo_out, loss_out):
    f_in = gwh_out.shape[1]
    toff = tail_offset(f_in)
    gwh_out[...] = packed[:, 0:f_in]
    gwo_out[...] = packed[0:CLS, toff:toff + 16]
    loss_out[...] = packed[15:16, toff:toff + 1]


def device_step(R, adj, feat, w_hidden, w_output, labels, train_mask, block_mask):
    NC = R * R * R
    f_in, hid = w_hidden.shape
    width = -(-(tail_offset(f_in) + 16) // B) * B
    any_spec = pl.BlockSpec(memory_space=pl.ANY)
    vmem_spec = pl.BlockSpec(memory_space=pltpu.VMEM)
    packed = pl.pallas_call(
        functools.partial(kernel, R),
        out_shape=pltpu.VMEM((hid, width), F32),
        in_specs=[any_spec] * 7,
        out_specs=vmem_spec,
        scratch_shapes=[
            pltpu.VMEM((2 * B, NC * B), BF),
            pltpu.VMEM((f_in, B), BF),
            pltpu.VMEM((hid, f_in), F32),
            pltpu.VMEM((CLS, hid), F32),
            pltpu.VMEM((8, hid), F32),
            pltpu.VMEM((1, 2 * B), jnp.int32),
            pltpu.VMEM((1, 2 * B), jnp.int32),
            pltpu.SMEM((8, block_mask.shape[1]), jnp.int32),
            pltpu.VMEM((hid, NC * B), BF),
            pltpu.VMEM((8, NC * B), BF),
            pltpu.VMEM((2, 16, B), F32),
            pltpu.VMEM((16, B), F32),
            pltpu.VMEM((8, 2 * B), F32),
            pltpu.VMEM((8, 2 * B), F32),
            pltpu.VMEM((8, 2 * B), BF),
            pltpu.VMEM((16, 2 * B), BF),
            pltpu.VMEM((NC, 8, B), F32),
            pltpu.VMEM((NC, 8, B), F32),
            pltpu.VMEM((2, NC, 8, B), F32),
            pltpu.VMEM((2, NC, 8, B), F32),
            pltpu.VMEM((2, 8, width), F32),
            pltpu.VMEM((2 * R, 8, width), F32),
            pltpu.VMEM((8, width), F32),
            pltpu.VMEM((R, 8, width), F32),
            pltpu.VMEM((8, width), F32),
            pltpu.VMEM((2 * R, 8, width), F32),
            pltpu.SemaphoreType.DMA((6,)),
            pltpu.SemaphoreType.DMA((2,)),
            pltpu.SemaphoreType.DMA,
            pltpu.SemaphoreType.DMA((5,)),
            pltpu.SemaphoreType.DMA((5,)),
            pltpu.SemaphoreType.DMA((5,)),
            pltpu.SemaphoreType.DMA((5, R)),
            pltpu.SemaphoreType.DMA((3, 6)),
            pltpu.SemaphoreType.DMA((3, 6)),
        ],
        compiler_params=pltpu.CompilerParams(collective_id=0, has_side_effects=True, vmem_limit_bytes=60 * 1024 * 1024),
        name='gcn_step',
    )(adj, feat.T, w_hidden.T, w_output.T, labels.reshape(1, -1), train_mask.reshape(1, -1), block_mask)
    gwh, gwo, loss = pl.pallas_call(
        unpack,
        out_shape=(jax.ShapeDtypeStruct((hid, f_in), F32), jax.ShapeDtypeStruct((CLS, hid), F32), jax.ShapeDtypeStruct((1, 1), F32)),
        in_specs=[vmem_spec],
        out_specs=(vmem_spec, vmem_spec, vmem_spec),
        name='gcn_unpack',
    )(pltpu.with_memory_space_constraint(packed, pltpu.VMEM))
    return loss[0, 0], gwh.T, gwo.T


def solution(mesh):
    row_spec = P(AXIS, None)
    vec_spec = P(AXIS)
    R = 4 if mesh.shape[AXIS] == 128 else 2
    return jax.shard_map(functools.partial(device_step, R), mesh=mesh,
                         in_specs=(row_spec, row_spec, P(), P(), vec_spec, vec_spec, P()), out_specs=(P(), P(), P()), check_vma=False)
```

time: 61.7 us -> 56.5 us (0.916)
  Pallas kernels: 58.4 us -> 55.7 us
  local copies, waits for them, and re-layouts: 1.24 us -> 0 us
  between operations: 1.8 us -> 0.64 us
    pallas_call x1 -> x2, Pallas kernels: 58.4 us -> 55.7 us  [the longest x1 55.1 us: device_step(): pl.pallas_call(functools.partial(kernel, R), out_shape=pltpu.VMEM((hid, w...]
    unnamed x2 -> x0, local copies, waits for them, and re-layouts: 1.24 us -> none
where the time goes in v3:
time: 56.5 us; the launch traced here: 56.4 us
  Pallas kernels  55.7 us (99%)
  between operations  0.64 us (1%)
    pallas_call x1, Pallas kernels, device_step(): pl.pallas_call(functools.partial(kernel, R), out_shape=pltpu.VMEM((hid, w...  55.1 us

profile of v3, /device:TPU:1, one launch (start us, length us, event | category | flops | bytes accessed | tf_op | source)
XLA Modules:
  0.0 56.4 jit_solution(13370668240072142858)
XLA Ops:
  0.6 55.1 %gcn_step.1.packed = f32[16,1536]{1,0:T(8,128)S(1)} custom-call(bf16[128,16384]{1,0:T(8,128)(2,1)} %adj.1, bf16[1433,128]{1,0:T(8,128)(2,1)} %bitcast.8, f32[16,1433]{1,0:T(8,128)} %bitcast.9, f32[7,16]{1,0:T(8,128)} %bitcast.10, s32[1,128]{1,0:T(1,128)} %bitcast.11, s32[1,128]{1,0:T(1,128)} %bitcast.12, s32[128,128]{1,0:T(8,128)} %bmask.1), custom_call_target="tpu_custom_call" | custom-call | tf_op jit(solution)/shard_map/gcn_step/pallas_call | solution.py:361
  55.7 0.7 %gcn_unpack.1 = (f32[16,1433]{1,0:T(8,128)}, f32[7,16]{1,0:T(8,128)}, f32[1,1]{1,0:T(1,128)}) custom-call(f32[16,1536]{1,0:T(8,128)S(1)} %gcn_step.1.packed), custom_call_target="tpu_custom_call" | custom-call | tf_op jit(solution)/shard_map/gcn_unpack/pallas_call | solution.py:406
